TPU v7x, 32 devices: a whole 2x2x4 slice. The times are simulated.
32 devices in a mesh: cell: 8 (over z, x), grp: 4 (over y, core).
Axes of the slice: x: 2, y: 2, z: 4, core: 2. Of those that a mesh axis runs over, the one named last changes fastest.
Arguments:
- atom_sites: float32 [3, 16384], P(None, ('cell', 'grp')), may hold values from 0 to 8, as said below
- grid_points: float32 [3, 12288], P(None, ('cell', 'grp')), may hold values from 0 to 8, as said below
- dipole_guess: float32 [3, 16384], P(None, ('cell', 'grp')), may hold values from -2 to 2
- fixed_field: float32 [3, 16384], P(None, ('cell', 'grp')), may hold values from -1800 to 1800
- polarisability: float32 [16384], P(('cell', 'grp')), may hold values from 0.0005 to 0.002
- base_charge: float32 [12288], P(('cell', 'grp')), may hold values from -12 to 12
- response: float32 [12288], P(('cell', 'grp')), may hold values from 0.02 to 0.2
- near_blocks: int32 [128, 8], P(('cell', 'grp')), may hold values from 0 to 47, as said below
- grid_blocks: int32 [128, 4], P(('cell', 'grp')), may hold values from 0 to 35, as said below
- source_blocks: int32 [96, 8], P(('cell', 'grp')), may hold values from 0 to 47, as said below
Outputs:
- dipoles: float32 [3, 16384], P(None, ('cell', 'grp'))
- qm_charges: float32 [12288], P(('cell', 'grp'))
Inputs may be any that keep to these rules, and one draw needn't show every extreme that they name: `atom_sites`: atom a has first coordinate in [c, c + 1) with c = a // 2048, the other two in [0, 1). `grid_points`: grid point g has first coordinate in [c, c + 1) with c = g // 1536, the other two in [0, 1). `near_blocks`: each row holds 8 distinct MM window indices, never the block's own index 16 + b % 16. `grid_blocks`: each row holds 4 distinct grid window indices. `source_blocks`: each row holds 8 distinct MM window indices.
All inputs are finite; a program needn't handle non-finite values.
Results may differ from a plain program's by a relative error of at most 0.0003.
Values sent between devices are 32-bit elements; how exact they have to be, the bound alone decides.
A program may use at most 64 MiB of HBM per device.

v0:
```python
import jax
import jax.numpy as jnp
from jax import lax
from jax.sharding import PartitionSpec as P

BLOCK = 128
ITERS = 3


soften_sq = 0.04


def with_halo(x, sides, width):
    for axis, dim in sides:
        peers, length = (lax.axis_size(axis), x.shape[dim])
        up = [(i, (i + 1) % peers) for i in range(peers - 1)]
        down = [(j, i) for i, j in up]
        last = lax.slice_in_dim(x, length - width, length, axis=dim)
        initial = lax.slice_in_dim(x, 0, width, axis=dim)
        before = lax.ppermute(last, axis, up)
        after = lax.ppermute(initial, axis, down)
        x = jnp.concatenate([before, x, after], axis=dim)
    return x


def pair_geometry(targets, sources):
    delta_x = targets[0][:, None] - sources[0][None, :]
    delta_y = targets[1][:, None] - sources[1][None, :]
    delta_z = targets[2][:, None] - sources[2][None, :]
    inverse = 1.0 / jnp.sqrt(delta_x * delta_x + delta_y * delta_y + delta_z * delta_z + soften_sq)
    inv_cube = inverse * inverse * inverse
    return (delta_x, delta_y, delta_z, inv_cube, inv_cube * inverse * inverse)


def dipole_field(targets, sources, moments, keep_mask):
    delta_x, delta_y, delta_z, inv_cube, inv_fifth = pair_geometry(targets, sources)
    projected = (
        moments[0][None, :] * delta_x
        + moments[1][None, :] * delta_y
        + moments[2][None, :] * delta_z
    )
    radial = 3.0 * projected * inv_fifth * keep_mask
    direct = inv_cube * keep_mask
    return jnp.stack(
        [
            jnp.sum(radial * delta_x - moments[0][None, :] * direct, axis=1),
            jnp.sum(radial * delta_y - moments[1][None, :] * direct, axis=1),
            jnp.sum(radial * delta_z - moments[2][None, :] * direct, axis=1),
        ]
    )


def charge_field(targets, sources, charges):
    delta_x, delta_y, delta_z, inv_cube, inv_fifth = pair_geometry(targets, sources)
    weight = charges[None, :] * inv_cube
    return jnp.stack(
        [
            jnp.sum(weight * delta_x, axis=1),
            jnp.sum(weight * delta_y, axis=1),
            jnp.sum(weight * delta_z, axis=1),
        ]
    )


def dipole_potential(targets, sources, moments):
    delta_x, delta_y, delta_z, inv_cube, inv_fifth = pair_geometry(targets, sources)
    projected = (
        moments[0][None, :] * delta_x
        + moments[1][None, :] * delta_y
        + moments[2][None, :] * delta_z
    )
    return jnp.sum(projected * inv_cube, axis=1)


def far_geometry(targets, cell_here, cell_count):
    centres = jnp.arange(cell_count, dtype=jnp.int32).astype(jnp.float32) + 0.5
    delta_x = targets[0][None, :] - centres[:, None]
    delta_y = targets[1][None, :] - 0.5
    delta_z = targets[2][None, :] - 0.5
    far_mask = (jnp.abs(jnp.arange(cell_count, dtype=jnp.int32) - cell_here) >= 2).astype(
        jnp.float32
    )[:, None]
    inverse = 1.0 / jnp.sqrt(delta_x * delta_x + delta_y * delta_y + delta_z * delta_z + soften_sq)
    inv_cube = inverse * inverse * inverse * far_mask
    return (delta_x, delta_y, delta_z, inv_cube, inv_cube * inverse * inverse)


def far_field(targets, cell_here, moments, charges):
    delta_x, delta_y, delta_z, inv_cube, inv_fifth = far_geometry(
        targets, cell_here, charges.shape[0]
    )
    projected = moments[:, 0:1] * delta_x + moments[:, 1:2] * delta_y + moments[:, 2:3] * delta_z
    radial = 3.0 * projected * inv_fifth
    coulomb = charges[:, None] * inv_cube
    return jnp.stack(
        [
            jnp.sum(radial * delta_x - moments[:, 0:1] * inv_cube + coulomb * delta_x, axis=0),
            jnp.sum(radial * delta_y - moments[:, 1:2] * inv_cube + coulomb * delta_y, axis=0),
            jnp.sum(radial * delta_z - moments[:, 2:3] * inv_cube + coulomb * delta_z, axis=0),
        ]
    )


def far_potential(targets, cell_here, moments):
    delta_x, delta_y, delta_z, inv_cube, inv_fifth = far_geometry(
        targets, cell_here, moments.shape[0]
    )
    projected = moments[:, 0:1] * delta_x + moments[:, 1:2] * delta_y + moments[:, 2:3] * delta_z
    return jnp.sum(projected * inv_cube, axis=0)


def listed_tiles(tile_set, index_lists):
    taken = jnp.take(tile_set, index_lists, axis=1)
    count, listed = index_lists.shape
    return jnp.transpose(taken, (1, 0, 2, 3)).reshape(count, 3, listed * tile_set.shape[2])


def spread(payload):
    lifted = payload[:, None, None, :]
    with_rims = with_halo(lifted, (("cell", 1),), 1)
    return lax.all_gather(with_rims, "grp", axis=2, tiled=True)


def body(
    atom_sites,
    grid_points,
    dipole_guess,
    fixed_field,
    polarisability,
    base_charge,
    response,
    near_blocks,
    grid_blocks,
    source_blocks,
):
    groups = lax.axis_size("grp")
    cell_here = lax.axis_index("cell")
    grp_here = lax.axis_index("grp")
    local_blocks = near_blocks.shape[0]
    local_gblocks = source_blocks.shape[0]
    atom_count = atom_sites.shape[1]
    grid_count = grid_points.shape[1]
    cell_blocks = local_blocks * groups
    cell_gblocks = local_gblocks * groups
    statics = spread(jnp.concatenate([atom_sites, grid_points], axis=1))
    site_tiles = statics[:, :, :, :atom_count].reshape(3, 3 * cell_blocks, BLOCK)
    point_tiles = statics[:, :, :, atom_count:].reshape(3, 3 * cell_gblocks, BLOCK)
    atom_targets = jnp.transpose(atom_sites.reshape(3, local_blocks, BLOCK), (1, 0, 2))
    grid_targets = jnp.transpose(grid_points.reshape(3, local_gblocks, BLOCK), (1, 0, 2))
    own_slots = cell_blocks + grp_here * local_blocks + jnp.arange(local_blocks, dtype=jnp.int32)
    atom_lists = jnp.concatenate([own_slots[:, None], near_blocks], axis=1)
    near_sites = listed_tiles(site_tiles, atom_lists)
    grid_sites = listed_tiles(point_tiles, grid_blocks)
    source_sites = listed_tiles(site_tiles, source_blocks)
    keep_mask = jnp.concatenate(
        [
            1.0 - jnp.eye(BLOCK, dtype=jnp.float32),
            jnp.ones((BLOCK, near_blocks.shape[1] * BLOCK), jnp.float32),
        ],
        axis=1,
    )
    centre = jnp.stack(
        [
            cell_here.astype(jnp.float32) + 0.5,
            jnp.array(0.5, jnp.float32),
            jnp.array(0.5, jnp.float32),
        ]
    )
    offsets = grid_points - centre[:, None]
    dipoles = dipole_guess
    charges = base_charge
    for iteration in range(ITERS):
        shared = spread(jnp.concatenate([dipoles, charges.reshape(3, grid_count // 3)], axis=1))
        dipole_tiles = shared[:, :, :, :atom_count].reshape(3, 3 * cell_blocks, BLOCK)
        charge_tiles = jnp.transpose(shared[:, :, :, atom_count:], (1, 2, 0, 3)).reshape(
            3 * cell_gblocks, BLOCK
        )
        local_sums = jnp.concatenate(
            [
                jnp.sum(dipoles, axis=1),
                jnp.sum(charges)[None],
                jnp.sum(charges[None, :] * offsets, axis=1),
            ]
        )
        cell_sums = lax.psum(local_sums, "grp")
        moment_table = lax.all_gather(cell_sums[None, :], "cell", axis=0, tiled=True)
        dipole_sums = moment_table[:, 0:3]
        charge_sums = moment_table[:, 3]
        moments = dipole_sums + moment_table[:, 4:7]
        near_dipoles = listed_tiles(dipole_tiles, atom_lists)
        source_dipoles = listed_tiles(dipole_tiles, source_blocks)
        grid_charges = jnp.take(charge_tiles, grid_blocks, axis=0).reshape(local_blocks, -1)

        def one_atom_block(block_args):
            targets, sources, source_moments, points, point_charges = block_args
            accumulated = dipole_field(targets, sources, source_moments, keep_mask)
            accumulated = accumulated + charge_field(targets, points, point_charges)
            return accumulated + far_field(targets, cell_here, moments, charge_sums)

        def one_grid_block(block_args):
            targets, sources, source_moments = block_args
            return dipole_potential(targets, sources, source_moments) + far_potential(
                targets, cell_here, dipole_sums
            )

        induced_field = lax.map(
            one_atom_block, (atom_targets, near_sites, near_dipoles, grid_sites, grid_charges)
        )
        induced_field = jnp.transpose(induced_field, (1, 0, 2)).reshape(3, atom_count)
        potential = lax.map(one_grid_block, (grid_targets, source_sites, source_dipoles)).reshape(
            grid_count
        )
        dipoles = polarisability[None, :] * (fixed_field + induced_field)
        charges = base_charge - response * potential
    return (dipoles, charges)


def solution(mesh):
    return jax.shard_map(
        body,
        mesh=mesh,
        in_specs=(
            P(None, ("cell", "grp")),
            P(None, ("cell", "grp")),
            P(None, ("cell", "grp")),
            P(None, ("cell", "grp")),
            P(("cell", "grp")),
            P(("cell", "grp")),
            P(("cell", "grp")),
            P(("cell", "grp"), None),
            P(("cell", "grp"), None),
            P(("cell", "grp"), None),
        ),
        out_specs=(P(None, ("cell", "grp")), P(("cell", "grp"))),
        check_vma=False,
    )
```

profile of v0, /device:TPU:0, one launch (start us, length us, event | category | flops | bytes accessed | tf_op | source)
XLA Modules:
  0.0 166.5 jit_solution(10735519480641597523)
XLA Ops:
  0.6 0.7 maximum_bitcast_fusion.1
  1.4 1.3 collective-permute-start.1
  2.7 5.5 %collective-permute-start = (f32[3,1,1,640]{3,0,2,1:T(4,128)S(1)}, f32[3,1,1,640]{3,0,2,1:T(4,128)S(1)}, u32[]{:S(2)}, u32[]{:S(2)}) collective-permute-start(f32[3,1,1,640]{3,0,2,1:T(4,128)S(1)} %maximum_bitcast_fusion.1), channel_id=1, source_target_pairs={{0,4},{4,8},{8,12},{12,16},{16,20},{20,24},{24,28},{1,5},{5,9},{9,... | collective-permute-start | bytes 23048 | tf_op jit(solution)/shard_map/ppermute | solution.py:20
  8.2 1.3 collective-permute-start.3
  9.5 5.4 %collective-permute-start.2 = (f32[3,1,1,896]{3,0,2,1:T(4,128)S(1)}, f32[3,1,1,896]{3,0,2,1:T(4,128)S(1)}, u32[]{:S(2)}, u32[]{:S(2)}) collective-permute-start(f32[3,1,1,896]{3,0,2,1:T(4,128)S(1)} %maximum_bitcast_fusion), channel_id=1, source_target_pairs={{0,4},{4,8},{8,12},{12,16},{16,20},{20,24},{24,28},{1,5},{5,9},{9,... | collective-permute-start | bytes 32264 | tf_op jit(solution)/shard_map/ppermute | solution.py:20
  15.0 0.7 copy-done.8
  15.8 0.7 copy-done.2
  16.4 0.6 reduce_sum.511
  17.3 0.7 maximum_bitcast_fusion.4
  18.0 5.7 %psum.21 = f32[1,7]{1,0:T(1,128)S(1)} all-reduce(f32[1,7]{1,0:T(1,128)S(1)} %maximum_bitcast_fusion.4), channel_id=1, replica_groups=mesh['cell'=8,'grp'=4] {'grp'}, use_global_device_ids=true, to_apply=%region_3.6 | all-reduce | flops 7 | bytes 56 | tf_op jit(solution)/shard_map/psum | solution.py:185
  23.8 0.7 copy-done.9
  24.8 19.3 %all-gather = f32[8,1,7]{2,1,0:T(1,128)S(1)} all-gather(f32[1,1,7]{2,1,0:T(1,128)S(1)} %bitcast.636), channel_id=1, replica_groups=mesh['cell'=8,'grp'=4] {'cell'}, dimensions={0}, use_global_device_ids=true | all-gather | bytes 252 | tf_op jit(solution)/shard_map/all_gather | solution.py:186
  44.6 5.4 %all_gather.21 = f32[3,3,4,640]{3,0,2,1:T(4,128)S(1)} all-gather(f32[3,3,1,640]{3,0,2,1:T(4,128)S(1)} %pad_maximum_fusion.1), channel_id=1, replica_groups=mesh['cell'=8,'grp'=4] {'grp'}, dimensions={2}, use_global_device_ids=true | all-gather | bytes 115200 | tf_op jit(solution)/shard_map/all_gather | solution.py:121
  50.0 0.6 gather_fusion.3
  50.7 0.6 gather_fusion.4
  51.3 0.6 gather_fusion.1
  51.9 5.6 %all_gather.22 = f32[3,3,4,896]{3,0,2,1:T(4,128)S(1)} all-gather(f32[3,3,1,896]{3,0,2,1:T(4,128)S(1)} %pad_maximum_fusion), channel_id=1, replica_groups=mesh['cell'=8,'grp'=4] {'grp'}, dimensions={2}, use_global_device_ids=true | all-gather | bytes 161280 | tf_op jit(solution)/shard_map/all_gather | solution.py:121
  57.5 0.6 gather_fusion.5
  58.1 0.6 gather_fusion.2
  58.8 0.6 gather_fusion
  59.7 2.4 %while.79 = (s32[]{:T(128)}, f32[3,128]{1,0:T(4,128)S(1)}, f32[3,3,1024]{2,0,1:T(4,128)S(1)}, f32[3,3,128]{2,1,0:T(4,128)S(1)}, f32[3,3,1024]{2,1,0:T(4,128)S(1)...) while((s32[]{:T(128)}, f32[3,128]{1,0:T(4,128)S(1)}, ...), condition=%wide.region_18.22_spmd, body=%wide.region_15.21_spmd.sunk | while | flops 2375092 | bytes 91217 | solution.py:210
  59.9 0.5 fusion.211
  62.1 0.6 fusion.190
  63.1 6.3 %while.78 = (s32[]{:T(128)}, f32[4,3,128]{2,1,0:T(4,128)S(1)}, f32[4,3,1152]{2,1,0:T(4,128)S(1)}, f32[4,3,128]{2,1,0:T(4,128)S(1)}, f32[4,3,1152]{2,1,0:T(4,128)...) while((s32[]{:T(128)}, f32[4,3,128]{2,1,0:T(4,128)S(1)}, ...), condition=%wide.region_14.17_spmd, body=%wide.region_4.16_spmd.sunk | while | flops 6232500 | bytes 724117 | solution.py:206
  63.7 0.9 fusion.208
  65.3 0.9 fusion.208
  66.9 0.9 fusion.208
  68.5 0.9 fusion.208
  69.6 1.3 collective-permute-start.5
  70.9 0.7 maximum_bitcast_fusion.5
  71.5 4.5 %collective-permute-start.4 = (f32[3,1,1,640]{3,0,2,1:T(4,128)S(1)}, f32[3,1,1,640]{3,0,2,1:T(4,128)S(1)}, u32[]{:S(2)}, u32[]{:S(2)}) collective-permute-start(f32[3,1,1,640]{3,0,2,1:T(4,128)S(1)} %maximum_bitcast_fusion.2), channel_id=1, source_target_pairs={{0,4},{4,8},{8,12},{12,16},{16,20},{20,24},{24,28},{1,5},{5,9},{9,... | collective-permute-start | bytes 23048 | tf_op jit(solution)/shard_map/ppermute | solution.py:20
  76.1 7.0 %psum.22 = f32[1,7]{1,0:T(1,128)S(1)} all-reduce(f32[1,7]{1,0:T(1,128)S(1)} %maximum_bitcast_fusion.5), channel_id=1, replica_groups=mesh['cell'=8,'grp'=4] {'grp'}, use_global_device_ids=true, to_apply=%region_22.26 | all-reduce | flops 7 | bytes 56 | tf_op jit(solution)/shard_map/psum | solution.py:185
  83.1 16.3 %all-gather.1 = f32[8,1,7]{2,1,0:T(1,128)S(1)} all-gather(f32[1,1,7]{2,1,0:T(1,128)S(1)} %bitcast.637), channel_id=1, replica_groups=mesh['cell'=8,'grp'=4] {'cell'}, dimensions={0}, use_global_device_ids=true | all-gather | bytes 252 | tf_op jit(solution)/shard_map/all_gather | solution.py:186
  99.8 5.4 %all_gather.24 = f32[3,3,4,640]{3,0,2,1:T(4,128)S(1)} all-gather(f32[3,3,1,640]{3,0,2,1:T(4,128)S(1)} %pad_maximum_fusion.2), channel_id=1, replica_groups=mesh['cell'=8,'grp'=4] {'grp'}, dimensions={2}, use_global_device_ids=true | all-gather | bytes 115200 | tf_op jit(solution)/shard_map/all_gather | solution.py:121
  105.3 0.6 gather_fusion.8
  105.9 0.6 gather_fusion.6
  106.5 0.6 gather_fusion.7
  107.3 6.3 %while.80 = (s32[]{:T(128)}, f32[4,3,128]{2,1,0:T(4,128)S(1)}, f32[4,3,1152]{2,1,0:T(4,128)S(1)}, f32[4,3,128]{2,1,0:T(4,128)S(1)}, f32[4,3,1152]{2,1,0:T(4,128)...) while((s32[]{:T(128)}, f32[4,3,128]{2,1,0:T(4,128)S(1)}, ...), condition=%wide.region_33.37_spmd, body=%wide.region_23.36_spmd.sunk | while | flops 6232500 | bytes 724117 | solution.py:206
  108.0 0.9 fusion.213
  109.6 0.9 fusion.213
  111.2 0.9 fusion.213
  112.8 0.9 fusion.213
  113.8 2.4 %while.81 = (s32[]{:T(128)}, f32[3,128]{1,0:T(4,128)S(1)}, f32[3,3,1024]{2,0,1:T(4,128)S(1)}, f32[3,3,128]{2,1,0:T(4,128)S(1)}, f32[3,3,1024]{2,1,0:T(4,128)S(1)...) while((s32[]{:T(128)}, f32[3,128]{1,0:T(4,128)S(1)}, ...), condition=%wide.region_37.41_spmd, body=%wide.region_34.40_spmd.sunk | while | flops 2375092 | bytes 91217 | solution.py:210
  114.1 0.5 fusion.216
  114.9 0.5 fusion.216
  115.7 0.5 fusion.216
  116.3 0.6 fusion.186
  117.1 1.3 collective-permute-start.7
  118.4 0.7 maximum_bitcast_fusion.6
  119.1 4.5 %collective-permute-start.6 = (f32[3,1,1,640]{3,0,2,1:T(4,128)S(1)}, f32[3,1,1,640]{3,0,2,1:T(4,128)S(1)}, u32[]{:S(2)}, u32[]{:S(2)}) collective-permute-start(f32[3,1,1,640]{3,0,2,1:T(4,128)S(1)} %maximum_bitcast_fusion.3), channel_id=1, source_target_pairs={{0,4},{4,8},{8,12},{12,16},{16,20},{20,24},{24,28},{1,5},{5,9},{9,... | collective-permute-start | bytes 23048 | tf_op jit(solution)/shard_map/ppermute | solution.py:20
  123.6 5.8 %psum.23 = f32[1,7]{1,0:T(1,128)S(1)} all-reduce(f32[1,7]{1,0:T(1,128)S(1)} %maximum_bitcast_fusion.6), channel_id=1, replica_groups=mesh['cell'=8,'grp'=4] {'grp'}, use_global_device_ids=true, to_apply=%region_41.45 | all-reduce | flops 7 | bytes 56 | tf_op jit(solution)/shard_map/psum | solution.py:185
  129.4 19.2 %all-gather.2 = f32[8,1,7]{2,1,0:T(1,128)S(1)} all-gather(f32[1,1,7]{2,1,0:T(1,128)S(1)} %bitcast.638), channel_id=1, replica_groups=mesh['cell'=8,'grp'=4] {'cell'}, dimensions={0}, use_global_device_ids=true | all-gather | bytes 252 | tf_op jit(solution)/shard_map/all_gather | solution.py:186
  149.0 5.4 %all_gather.26 = f32[3,3,4,640]{3,0,2,1:T(4,128)S(1)} all-gather(f32[3,3,1,640]{3,0,2,1:T(4,128)S(1)} %pad_maximum_fusion.3), channel_id=1, replica_groups=mesh['cell'=8,'grp'=4] {'grp'}, dimensions={2}, use_global_device_ids=true | all-gather | bytes 115200 | tf_op jit(solution)/shard_map/all_gather | solution.py:121
  154.4 0.6 gather_fusion.11
  155.0 0.6 gather_fusion.9
  155.6 0.6 gather_fusion.10
  156.5 6.3 %while.82 = (s32[]{:T(128)}, f32[4,3,128]{2,1,0:T(4,128)S(1)}, f32[4,3,1152]{2,1,0:T(4,128)S(1)}, f32[4,3,128]{2,1,0:T(4,128)S(1)}, f32[4,3,1152]{2,1,0:T(4,128)...) while((s32[]{:T(128)}, f32[4,3,128]{2,1,0:T(4,128)S(1)}, ...), condition=%wide.region_52.56_spmd, body=%wide.region_42.55_spmd.sunk | while | flops 6232500 | bytes 724117 | solution.py:206
  157.2 0.9 fusion.218
  158.7 0.9 fusion.218
  160.3 0.9 fusion.218
  161.9 0.9 fusion.218
  162.8 0.6 fusion.178
  163.5 2.4 %while.83 = (s32[]{:T(128)}, f32[3,128]{1,0:T(4,128)S(1)}, f32[3,3,1024]{2,0,1:T(4,128)S(1)}, f32[3,3,128]{2,1,0:T(4,128)S(1)}, f32[3,3,1024]{2,1,0:T(4,128)S(1)...) while((s32[]{:T(128)}, f32[3,128]{1,0:T(4,128)S(1)}, ...), condition=%wide.region_56.60_spmd, body=%wide.region_53.59_spmd.sunk | while | flops 2375092 | bytes 91217 | solution.py:210
  165.9 0.6 fusion.181
  (354 shorter events, 15.7 us)
Async XLA Ops:
  0.6 7.5 %copy-start = (f32[3,384]{1,0:T(4,128)S(1)}, f32[3,384]{1,0:T(4,128)}, u32[]{:S(2)}) copy-start(f32[3,384]{1,0:T(4,128)} %param.29) | copy-start | bytes 13828
  0.6 7.5 %copy-start.1 = (f32[3,512]{1,0:T(4,128)S(1)}, f32[3,512]{1,0:T(4,128)}, u32[]{:S(2)}) copy-start(f32[3,512]{1,0:T(4,128)} %param.28) | copy-start | bytes 18436
  1.4 43.2 %collective-permute-start.1 = (f32[3,1,1,640]{3,0,2,1:T(4,128)S(1)}, f32[3,1,1,640]{3,0,2,1:T(4,128)S(1)}, u32[]{:S(2)}, u32[]{:S(2)}) collective-permute-start(f32[3,1,1,640]{3,0,2,1:T(4,128)S(1)} %maximum_bitcast_fusion.1), channel_id=1, source_target_pairs={{4,0},{8,4},{12,8},{16,12},{20,16},{24,20},{28,24},{5,1},{9,5},{13... | collective-permute-start | bytes 23048 | tf_op jit(solution)/shard_map/ppermute | solution.py:21
  2.7 41.9 %collective-permute-start = (f32[3,1,1,640]{3,0,2,1:T(4,128)S(1)}, f32[3,1,1,640]{3,0,2,1:T(4,128)S(1)}, u32[]{:S(2)}, u32[]{:S(2)}) collective-permute-start(f32[3,1,1,640]{3,0,2,1:T(4,128)S(1)} %maximum_bitcast_fusion.1), channel_id=1, source_target_pairs={{0,4},{4,8},{8,12},{12,16},{16,20},{20,24},{24,28},{1,5},{5,9},{9,... | collective-permute-start | bytes 23048 | tf_op jit(solution)/shard_map/ppermute | solution.py:20
  8.2 6.8 %copy-start.7 = (s32[4,4]{1,0:T(4,128)S(1)}, s32[4,4]{1,0:T(4,128)}, u32[]{:S(2)}) copy-start(s32[4,4]{1,0:T(4,128)} %param.36) | copy-start | bytes 196
  8.2 43.7 %collective-permute-start.3 = (f32[3,1,1,896]{3,0,2,1:T(4,128)S(1)}, f32[3,1,1,896]{3,0,2,1:T(4,128)S(1)}, u32[]{:S(2)}, u32[]{:S(2)}) collective-permute-start(f32[3,1,1,896]{3,0,2,1:T(4,128)S(1)} %maximum_bitcast_fusion), channel_id=1, source_target_pairs={{4,0},{8,4},{12,8},{16,12},{20,16},{24,20},{28,24},{5,1},{9,5},{13... | collective-permute-start | bytes 32264 | tf_op jit(solution)/shard_map/ppermute | solution.py:21
  9.5 42.4 %collective-permute-start.2 = (f32[3,1,1,896]{3,0,2,1:T(4,128)S(1)}, f32[3,1,1,896]{3,0,2,1:T(4,128)S(1)}, u32[]{:S(2)}, u32[]{:S(2)}) collective-permute-start(f32[3,1,1,896]{3,0,2,1:T(4,128)S(1)} %maximum_bitcast_fusion), channel_id=1, source_target_pairs={{0,4},{4,8},{8,12},{12,16},{16,20},{20,24},{24,28},{1,5},{5,9},{9,... | collective-permute-start | bytes 32264 | tf_op jit(solution)/shard_map/ppermute | solution.py:20
  15.0 0.7 copy-start.8
  15.7 0.7 copy-start.2
  15.7 1.3 copy-start.4
  23.8 0.7 copy-start.9
  59.6 2.4 %copy-start.5 = (f32[384]{0:T(512)S(1)}, f32[384]{0:T(512)}, u32[]{:S(2)}) copy-start(f32[384]{0:T(512)} %param.34) | copy-start | bytes 4612
  63.0 6.4 %copy-start.3 = (f32[3,512]{1,0:T(4,128)S(1)}, f32[3,512]{1,0:T(4,128)}, u32[]{:S(2)}) copy-start(f32[3,512]{1,0:T(4,128)} %param.31) | copy-start | bytes 18436
  63.0 6.4 %copy-start.6 = (f32[512]{0:T(512)S(1)}, f32[512]{0:T(512)}, u32[]{:S(2)}) copy-start(f32[512]{0:T(512)} %param.32) | copy-start | bytes 6148
  69.6 30.3 %collective-permute-start.5 = (f32[3,1,1,640]{3,0,2,1:T(4,128)S(1)}, f32[3,1,1,640]{3,0,2,1:T(4,128)S(1)}, u32[]{:S(2)}, u32[]{:S(2)}) collective-permute-start(f32[3,1,1,640]{3,0,2,1:T(4,128)S(1)} %maximum_bitcast_fusion.2), channel_id=1, source_target_pairs={{4,0},{8,4},{12,8},{16,12},{20,16},{24,20},{28,24},{5,1},{9,5},{13... | collective-permute-start | bytes 23048 | tf_op jit(solution)/shard_map/ppermute | solution.py:21
  71.5 28.3 %collective-permute-start.4 = (f32[3,1,1,640]{3,0,2,1:T(4,128)S(1)}, f32[3,1,1,640]{3,0,2,1:T(4,128)S(1)}, u32[]{:S(2)}, u32[]{:S(2)}) collective-permute-start(f32[3,1,1,640]{3,0,2,1:T(4,128)S(1)} %maximum_bitcast_fusion.2), channel_id=1, source_target_pairs={{0,4},{4,8},{8,12},{12,16},{16,20},{20,24},{24,28},{1,5},{5,9},{9,... | collective-permute-start | bytes 23048 | tf_op jit(solution)/shard_map/ppermute | solution.py:20
  117.1 31.9 %collective-permute-start.7 = (f32[3,1,1,640]{3,0,2,1:T(4,128)S(1)}, f32[3,1,1,640]{3,0,2,1:T(4,128)S(1)}, u32[]{:S(2)}, u32[]{:S(2)}) collective-permute-start(f32[3,1,1,640]{3,0,2,1:T(4,128)S(1)} %maximum_bitcast_fusion.3), channel_id=1, source_target_pairs={{4,0},{8,4},{12,8},{16,12},{20,16},{24,20},{28,24},{5,1},{9,5},{13... | collective-permute-start | bytes 23048 | tf_op jit(solution)/shard_map/ppermute | solution.py:21
  119.1 29.9 %collective-permute-start.6 = (f32[3,1,1,640]{3,0,2,1:T(4,128)S(1)}, f32[3,1,1,640]{3,0,2,1:T(4,128)S(1)}, u32[]{:S(2)}, u32[]{:S(2)}) collective-permute-start(f32[3,1,1,640]{3,0,2,1:T(4,128)S(1)} %maximum_bitcast_fusion.3), channel_id=1, source_target_pairs={{0,4},{4,8},{8,12},{12,16},{16,20},{20,24},{24,28},{1,5},{5,9},{9,... | collective-permute-start | bytes 23048 | tf_op jit(solution)/shard_map/ppermute | solution.py:20
where the time goes:
time: 167 us; the launch traced here: 166 us
  blocking collectives  95.1 us (57%)
  other arithmetic  30.4 us (18%)
  starting transfers between devices  25.2 us (15%)
  local copies, waits for them, and re-layouts  13.1 us (8%)
    all_gather x3, blocking collectives, body(): lax.all_gather(cell_sums[None, :], 'cell', axis=0, tiled=True)  54.8 us
    all_gather x4, blocking collectives, spread(): return lax.all_gather(with_rims, 'grp', axis=2, tiled=True)  21.7 us
    ppermute x4, starting transfers between devices, with_halo(): before = lax.ppermute(last, axis, up)  20 us
    psum x3, blocking collectives, body(): cell_sums = lax.psum(local_sums, 'grp')  18.6 us
    reduce_sum x12, other arithmetic, dipole_field(): jnp.sum(radial * delta_x - moments[0][None, :] * direct, axis=1)  10.7 us
    gather x10, local copies, waits for them, and re-layouts, listed_tiles(): taken = jnp.take(tile_set, index_lists, axis=1)  5.42 us
    ppermute x4, starting transfers between devices, with_halo(): after = lax.ppermute(initial, axis, down)  5.16 us
    reduce_sum x9, other arithmetic, dipole_potential(): return jnp.sum(projected * inv_cube, axis=1)  4.71 us
  transfers between devices with their start and end apart: 8, of which 0 were waited for; matrix products, arithmetic and copies ran while one was open for 4% of the time, Pallas kernels for 0%

commit v1 on v0

v1 whole, which is shorter than its diff:
```python
import functools
import math

import jax
import jax.numpy as jnp
from jax import lax
from jax.experimental import pallas as pl
from jax.experimental.pallas import tpu as pltpu
from jax.sharding import PartitionSpec as P

BLOCK = 128
SUB = 8
GROUPS = BLOCK // SUB
UNROLL = 8
HALVES = GROUPS // UNROLL
ITERS = 3
MESH = pl.DeviceIdType.MESH

soften_sq = 0.04


def round_up(n, m):
    return (n + m - 1) // m * m


def body(dims, *refs):
    cells, grps, na, ng, nb, nq, nm = dims
    near_s, grid_s, source_s, sites, points, guess, fixed, pol, base, resp = refs[:10]
    out_dip, out_q = refs[10:12]
    stat = refs[12]
    dyn = refs[13 : 13 + ITERS]
    tab = refs[13 + ITERS : 13 + 2 * ITERS]
    rest = refs[13 + 2 * ITERS :]
    tgt_a, tgt_g, geo, cgeo, pgeo, fld = rest[:6]
    stat_send, stat_recv, dyn_send, dyn_recv, far_send, far_recv = rest[6:]
    cell = lax.axis_index("cell")
    grp = lax.axis_index("grp")
    has_prev = cell > 0
    has_next = cell < cells - 1
    nk = nb + 1
    own = grps + grp
    cell_f = cell.astype(jnp.float32)
    centre = (cell_f + 0.5, 0.5, 0.5)

    def vec_row(ref, a, b):
        return ref[a : a + 1, b * BLOCK : (b + 1) * BLOCK]

    def flat_row(ref, b):
        return ref[b * BLOCK : (b + 1) * BLOCK].reshape(1, BLOCK)

    lanes = lax.broadcasted_iota(jnp.int32, (SUB, BLOCK), 1)
    subs = lax.broadcasted_iota(jnp.int32, (SUB, BLOCK), 0)
    diag = lanes - subs

    for it in range(ITERS):
        tab[it][...] = jnp.zeros_like(tab[it])

    @pl.when(jnp.logical_not(has_prev))
    def _():
        for p in range(grps):
            stat[p] = jnp.zeros(stat.shape[1:], jnp.float32)
            for it in range(ITERS):
                dyn[it][p] = jnp.zeros(dyn[it].shape[1:], jnp.float32)

    @pl.when(jnp.logical_not(has_next))
    def _():
        for p in range(2 * grps, 3 * grps):
            stat[p] = jnp.zeros(stat.shape[1:], jnp.float32)
            for it in range(ITERS):
                dyn[it][p] = jnp.zeros(dyn[it].shape[1:], jnp.float32)

    barrier = pltpu.get_barrier_semaphore()

    def greet(c, g):
        pl.semaphore_signal(barrier, inc=1, device_id=(c, g), device_id_type=MESH)

    def each_far(act):
        def step(c, carry):
            @pl.when(jnp.abs(c - cell) >= 2)
            def _():
                act(c)

            return carry

        lax.fori_loop(0, cells, step, 0)

    each_far(lambda c: greet(c, grp))

    @pl.when(has_prev)
    def _():
        for j in range(grps):
            greet(cell - 1, j)

    @pl.when(has_next)
    def _():
        for j in range(grps):
            greet(cell + 1, j)

    for d in range(1, grps):
        greet(cell, lax.rem(grp + d, grps))

    for a in range(3):
        for b in range(na):
            stat[own, a * na + b : a * na + b + 1, :] = vec_row(sites, a, b)
            dyn[0][own, a * na + b : a * na + b + 1, :] = vec_row(guess, a, b)
        for b in range(ng):
            r = 3 * na + a * ng + b
            stat[own, r : r + 1, :] = vec_row(points, a, b)
    for b in range(ng):
        dyn[0][own, 3 * na + b : 3 * na + b + 1, :] = flat_row(base, b)

    for a in range(3):
        for b in range(na):
            tgt_a[b, a] = jnp.transpose(jnp.broadcast_to(vec_row(sites, a, b), (BLOCK, BLOCK)))
        for b in range(ng):
            tgt_g[b, a] = jnp.transpose(jnp.broadcast_to(vec_row(points, a, b), (BLOCK, BLOCK)))

    def inverse_of(dx, dy, dz):
        return lax.rsqrt(dx * dx + dy * dy + dz * dz + soften_sq)

    def store_dipole_pair(slot, targets, source, self_mask):
        dx, dy, dz = (t - s for t, s in zip(targets, source))
        inv = inverse_of(dx, dy, dz)
        cube = inv * inv * inv
        weight = cube * lax.rsqrt(inv) * math.sqrt(3.0)
        geo[slot] = dx * weight
        geo[slot + 1] = dy * weight
        geo[slot + 2] = dz * weight
        geo[slot + 3] = cube if self_mask is None else jnp.where(self_mask, 0.0, cube)

    def store_charge_pair(ref, slot, targets, source):
        dx, dy, dz = (t - s for t, s in zip(targets, source))
        inv = inverse_of(dx, dy, dz)
        cube = inv * inv * inv
        ref[slot] = dx * cube
        ref[slot + 1] = dy * cube
        ref[slot + 2] = dz * cube

    def wide(row):
        return jnp.broadcast_to(row, (SUB, BLOCK))

    def targets_of(ref, b, group):
        return [ref[b, a, pl.ds(group * SUB, SUB), :] for a in range(3)]

    for b in range(na):
        source = [wide(vec_row(sites, a, b)) for a in range(3)]
        for t in range(GROUPS):
            slot = (b * GROUPS + t) * nk * 4
            store_dipole_pair(slot, targets_of(tgt_a, b, t), source, diag == t * SUB)

    greeted = grps - 1
    greeted += has_prev.astype(jnp.int32) * (grps - 1) + has_next.astype(jnp.int32) * (grps - 1)
    greeted += cells - 1
    pl.semaphore_wait(barrier, greeted)

    def piece_copy(buf, send, recv, slot, c, g):
        return pltpu.make_async_remote_copy(
            src_ref=buf.at[own],
            dst_ref=buf.at[slot * grps + grp],
            send_sem=send.at[slot * grps + g],
            recv_sem=recv.at[slot * grps + grp],
            device_id=(c, g),
            device_id_type=MESH,
        )

    def for_peers(buf, send, recv, act):
        for d in range(1, grps):
            g = lax.rem(grp + d, grps)
            act(piece_copy(buf, send, recv, 1, cell, g))

    def for_neighbours(buf, send, recv, act):
        @pl.when(has_prev)
        def _():
            for d in range(grps):
                g = lax.rem(grp + d, grps)
                act(piece_copy(buf, send, recv, 2, cell - 1, g))

        @pl.when(has_next)
        def _():
            for d in range(grps):
                g = lax.rem(grp + d, grps)
                act(piece_copy(buf, send, recv, 0, cell + 1, g))

    def arrival(buf, send, recv, p, c, g):
        pltpu.make_async_remote_copy(
            src_ref=buf.at[p],
            dst_ref=buf.at[p],
            send_sem=send.at[p],
            recv_sem=recv.at[p],
            device_id=(c, g),
            device_id_type=MESH,
        ).wait_recv()

    def peers_arrive(buf, send, recv):
        for d in range(1, grps):
            g = lax.rem(grp + d, grps)
            arrival(buf, send, recv, grps + g, cell, g)

    def neighbours_arrive(buf, send, recv):
        @pl.when(has_prev)
        def _():
            for g in range(grps):
                arrival(buf, send, recv, g, cell - 1, g)

        @pl.when(has_next)
        def _():
            for g in range(grps):
                arrival(buf, send, recv, 2 * grps + g, cell + 1, g)

    def start(copy):
        copy.start()

    def far_copy(it, c):
        return pltpu.make_async_remote_copy(
            src_ref=tab[it].at[cell],
            dst_ref=tab[it].at[cell],
            send_sem=far_send.at[it, c],
            recv_sem=far_recv.at[it, cell],
            device_id=(c, grp),
            device_id_type=MESH,
        )

    def far_arrival(it, c):
        pltpu.make_async_remote_copy(
            src_ref=tab[it].at[c],
            dst_ref=tab[it].at[c],
            send_sem=far_send.at[it, c],
            recv_sem=far_recv.at[it, c],
            device_id=(c, grp),
            device_id_type=MESH,
        ).wait_recv()

    def cell_sums(it):
        rows = []
        total = dyn[it][grps]
        for p in range(1, grps):
            total = total + dyn[it][grps + p]
        for a in range(3):
            rows.append(jnp.sum(total[a * na : (a + 1) * na], axis=0, keepdims=True))
        rows.append(jnp.sum(total[3 * na : 3 * na + ng], axis=0, keepdims=True))
        for a in range(3):
            moment = None
            for p in range(grps):
                q = dyn[it][grps + p, 3 * na : 3 * na + ng, :]
                r = 3 * na + a * ng
                term = q * (stat[grps + p, r : r + ng, :] - centre[a])
                moment = term if moment is None else moment + term
            rows.append(jnp.sum(moment, axis=0, keepdims=True))
        tile = jnp.zeros((SUB, BLOCK), jnp.float32)
        for n, row in enumerate(rows):
            tile = jnp.where(subs == n, wide(row), tile)
        sums = jnp.sum(tile, axis=1, keepdims=True)
        tab[it][cell] = jnp.broadcast_to(sums, (SUB, BLOCK))

    def mm_place(w):
        return lax.div(w, na), lax.rem(w, na)

    def grid_place(w):
        return lax.div(w, ng), lax.rem(w, ng)

    def site_rows(w):
        p, lb = mm_place(w)
        return [wide(stat[p, pl.ds(a * na + lb, 1), :]) for a in range(3)]

    def point_rows(w):
        p, lb = grid_place(w)
        return [wide(stat[p, pl.ds(3 * na + a * ng + lb, 1), :]) for a in range(3)]

    def geometry_atoms(i, carry):
        b = lax.div(i, HALVES)
        first = lax.rem(i, HALVES) * UNROLL
        for k in range(nb):
            source = site_rows(near_s[b, k])
            for t in range(UNROLL):
                slot = ((i * UNROLL + t) * nk + k + 1) * 4
                store_dipole_pair(slot, targets_of(tgt_a, b, first + t), source, None)
        for k in range(nq):
            source = point_rows(grid_s[b, k])
            for t in range(UNROLL):
                slot = ((i * UNROLL + t) * nq + k) * 3
                store_charge_pair(cgeo, slot, targets_of(tgt_a, b, first + t), source)
        return carry

    def geometry_grid(i, carry):
        b = lax.div(i, HALVES)
        first = lax.rem(i, HALVES) * UNROLL
        for k in range(nm):
            source = site_rows(source_s[b, k])
            for t in range(UNROLL):
                slot = ((i * UNROLL + t) * nm + k) * 3
                store_charge_pair(pgeo, slot, targets_of(tgt_g, b, first + t), source)
        return carry

    def near_atoms(it, i, carry):
        b = lax.div(i, HALVES)
        first = lax.rem(i, HALVES) * UNROLL
        acc = [[None] * 3 for _ in range(UNROLL)]
        for k in range(nk):
            p, lb = (own, b) if k == 0 else mm_place(near_s[b, k - 1])
            mu = [wide(dyn[it][p, pl.ds(a * na + lb, 1), :]) for a in range(3)]
            for t in range(UNROLL):
                slot = ((i * UNROLL + t) * nk + k) * 4
                u = [geo[slot + a] for a in range(3)]
                cube = geo[slot + 3]
                proj = u[0] * mu[0] + u[1] * mu[1] + u[2] * mu[2]
                for a in range(3):
                    term = u[a] * proj - cube * mu[a]
                    acc[t][a] = term if k == 0 else acc[t][a] + term
        for k in range(nq):
            p, lb = grid_place(grid_s[b, k])
            q = wide(dyn[it][p, pl.ds(3 * na + lb, 1), :])
            for t in range(UNROLL):
                slot = ((i * UNROLL + t) * nq + k) * 3
                for a in range(3):
                    acc[t][a] = acc[t][a] + cgeo[slot + a] * q
        out = []
        for a in range(3):
            row = jnp.zeros((SUB, BLOCK), jnp.float32)
            for t in range(UNROLL):
                total = jnp.sum(acc[t][a], axis=1, keepdims=True)
                row = jnp.where(diag == (first + t) * SUB, total, row)
            out.append(row)
        for a in range(3):
            fld[i * 3 + a] = out[a]
        return carry

    def near_grid(it, i, carry):
        b = lax.div(i, HALVES)
        first = lax.rem(i, HALVES) * UNROLL
        acc = [None] * UNROLL
        for k in range(nm):
            p, lb = mm_place(source_s[b, k])
            mu = [wide(dyn[it][p, pl.ds(a * na + lb, 1), :]) for a in range(3)]
            for t in range(UNROLL):
                slot = ((i * UNROLL + t) * nm + k) * 3
                term = pgeo[slot] * mu[0] + pgeo[slot + 1] * mu[1] + pgeo[slot + 2] * mu[2]
                acc[t] = term if k == 0 else acc[t] + term
        row = jnp.zeros((SUB, BLOCK), jnp.float32)
        for t in range(UNROLL):
            total = jnp.sum(acc[t], axis=1, keepdims=True)
            row = jnp.where(diag == (first + t) * SUB, total, row)
        fld[na * HALVES * 3 + i] = row
        return carry

    def far_geometry(row_of):
        c = lax.broadcasted_iota(jnp.int32, (cells, BLOCK), 0)
        dx = row_of(0) - (c.astype(jnp.float32) + 0.5)
        dy = jnp.broadcast_to(row_of(1) - 0.5, (cells, BLOCK))
        dz = jnp.broadcast_to(row_of(2) - 0.5, (cells, BLOCK))
        inv = inverse_of(dx, dy, dz)
        cube = jnp.where(jnp.abs(c - cell) >= 2, inv * inv * inv, 0.0)
        return (dx, dy, dz), cube, cube * inv * inv * 3.0

    def column_sum(x):
        return jnp.sum(x, axis=0, keepdims=True)

    for_peers(stat, stat_send, stat_recv, start)
    for_peers(dyn[0], dyn_send.at[0], dyn_recv.at[0], start)
    for_neighbours(stat, stat_send, stat_recv, start)
    for_neighbours(dyn[0], dyn_send.at[0], dyn_recv.at[0], start)
    peers_arrive(stat, stat_send, stat_recv)

    for it in range(ITERS):
        send, recv = dyn_send.at[it], dyn_recv.at[it]
        if it > 0:
            for_peers(dyn[it], send, recv, start)
            for_neighbours(dyn[it], send, recv, start)
        peers_arrive(dyn[it], send, recv)
        cell_sums(it)
        each_far(lambda c: far_copy(it, c).start())
        if it == 0:
            neighbours_arrive(stat, stat_send, stat_recv)
            lax.fori_loop(0, na * HALVES, geometry_atoms, 0)
            lax.fori_loop(0, ng * HALVES, geometry_grid, 0)
        neighbours_arrive(dyn[it], send, recv)
        lax.fori_loop(0, na * HALVES, functools.partial(near_atoms, it), 0)
        lax.fori_loop(0, ng * HALVES, functools.partial(near_grid, it), 0)
        each_far(lambda c: far_arrival(it, c))
        sums = [tab[it][:, n, :] for n in range(7)]
        moments = [sums[a] + sums[4 + a] for a in range(3)]
        for b in range(na):
            delta, cube, fifth = far_geometry(lambda a: vec_row(sites, a, b))
            radial = fifth * (moments[0] * delta[0] + moments[1] * delta[1] + moments[2] * delta[2])
            radial = radial + sums[3] * cube
            for a in range(3):
                far = column_sum(radial * delta[a] - moments[a] * cube)
                near = fld[b * HALVES * 3 + a]
                for h in range(1, HALVES):
                    near = near + fld[(b * HALVES + h) * 3 + a]
                new = flat_row(pol, b) * (vec_row(fixed, a, b) + (column_sum(near) + far))
                if it + 1 < ITERS:
                    dyn[it + 1][own, a * na + b : a * na + b + 1, :] = new
                else:
                    out_dip[a : a + 1, b * BLOCK : (b + 1) * BLOCK] = new
        for b in range(ng):
            delta, cube, _ = far_geometry(lambda a: vec_row(points, a, b))
            proj = sums[0] * delta[0] + sums[1] * delta[1] + sums[2] * delta[2]
            far = column_sum(proj * cube)
            slot = na * HALVES * 3 + b * HALVES
            near = fld[slot]
            for h in range(1, HALVES):
                near = near + fld[slot + h]
            new = flat_row(base, b) - flat_row(resp, b) * (column_sum(near) + far)
            if it + 1 < ITERS:
                dyn[it + 1][own, 3 * na + b : 3 * na + b + 1, :] = new
            else:
                out_q[b * BLOCK : (b + 1) * BLOCK] = new.reshape(BLOCK)

    def finish(copy):
        copy.wait_send()

    for_peers(stat, stat_send, stat_recv, finish)
    for_neighbours(stat, stat_send, stat_recv, finish)
    for it in range(ITERS):
        for_peers(dyn[it], dyn_send.at[it], dyn_recv.at[it], finish)
        for_neighbours(dyn[it], dyn_send.at[it], dyn_recv.at[it], finish)
        each_far(lambda c: far_copy(it, c).wait_send())


def solution(mesh):
    cells, grps = mesh.shape["cell"], mesh.shape["grp"]

    def step(sites, points, guess, fixed, pol, base, resp, near, grid, source):
        na, nb = near.shape
        nq = grid.shape[1]
        ng, nm = source.shape
        stat_rows = round_up(3 * na + 3 * ng, SUB)
        dyn_rows = round_up(3 * na + ng, SUB)
        f32 = jnp.float32
        smem = pl.BlockSpec(memory_space=pltpu.SMEM)
        vmem = pl.BlockSpec(memory_space=pltpu.VMEM)
        dma = pltpu.SemaphoreType.DMA
        return pl.pallas_call(
            functools.partial(body, (cells, grps, na, ng, nb, nq, nm)),
            out_shape=(
                jax.ShapeDtypeStruct(sites.shape, f32),
                jax.ShapeDtypeStruct(base.shape, f32),
            ),
            in_specs=[smem] * 3 + [vmem] * 7,
            out_specs=(vmem, vmem),
            scratch_shapes=[pltpu.VMEM((3 * grps, stat_rows, BLOCK), f32)]
            + [pltpu.VMEM((3 * grps, dyn_rows, BLOCK), f32) for _ in range(ITERS)]
            + [pltpu.VMEM((cells, SUB, BLOCK), f32) for _ in range(ITERS)]
            + [
                pltpu.VMEM((na, 3, BLOCK, BLOCK), f32),
                pltpu.VMEM((ng, 3, BLOCK, BLOCK), f32),
                pltpu.VMEM((na * GROUPS * (nb + 1) * 4, SUB, BLOCK), f32),
                pltpu.VMEM((na * GROUPS * nq * 3, SUB, BLOCK), f32),
                pltpu.VMEM((ng * GROUPS * nm * 3, SUB, BLOCK), f32),
                pltpu.VMEM(((na * 3 + ng) * HALVES, SUB, BLOCK), f32),
                dma((3 * grps,)),
                dma((3 * grps,)),
                dma((ITERS, 3 * grps)),
                dma((ITERS, 3 * grps)),
                dma((ITERS, cells)),
                dma((ITERS, cells)),
            ],
            compiler_params=pltpu.CompilerParams(collective_id=0, has_side_effects=True),
        )(near, grid, source, sites, points, guess, fixed, pol, base, resp)

    pair = P(("cell", "grp"))
    wide = P(None, ("cell", "grp"))
    tall = P(("cell", "grp"), None)
    return jax.shard_map(
        step,
        mesh=mesh,
        in_specs=(wide, wide, wide, wide, pair, pair, pair, tall, tall, tall),
        out_specs=(wide, pair),
        check_vma=False,
    )
```

time: 167 us -> 36.4 us (0.22)
  blocking collectives: 95.1 us -> 0 us
  Pallas kernels: 0 us -> 33.7 us
  other arithmetic: 30.4 us -> 0 us
  starting transfers between devices: 25.2 us -> 0 us
  local copies, waits for them, and re-layouts: 13.1 us -> 1.88 us
    all_gather x7 -> x0, blocking collectives: 76.5 us -> none  [the longest x3 54.8 us: body(): lax.all_gather(cell_sums[None, :], 'cell', axis=0, tiled=True)]
    pallas_call x0 -> x1, Pallas kernels: none -> 33.7 us  [step(): pl.pallas_call(functools.partial(body, (cells, grps, na, ng, nb, nq, nm))...]
    ppermute x8 -> x0, starting transfers between devices: 25.2 us -> none  [the longest x4 20 us: with_halo(): before = lax.ppermute(last, axis, up)]
    reduce_sum x63 -> x0, other arithmetic: 24.3 us -> none  [the longest x12 10.7 us: dipole_field(): jnp.sum(radial * delta_x - moments[0][None, :] * direct, axis=1)]
    psum x3 -> x0, blocking collectives: 18.6 us -> none  [body(): cell_sums = lax.psum(local_sums, 'grp')]
    gather x13 -> x0, local copies, waits for them, and re-layouts: 7.11 us -> none  [the longest x10 5.42 us: listed_tiles(): taken = jnp.take(tile_set, index_lists, axis=1)]
    broadcast_in_dim x7 -> x0, other arithmetic: 2.87 us -> none  [the longest x3 2.13 us: body(): cell_sums[None, :]]
    slice x50 -> x0, local copies, waits for them, and re-layouts: 1.78 us -> none  [the longest x21 1.09 us: pair_geometry(): delta_x = targets[0][:, None] - sources[0][None, :]]
  transfers between devices with their start and end apart: 8 -> 0, of which waited for: 0 -> 0; matrix products, arithmetic and copies ran while one was open for 4% -> 0% of each run, Pallas kernels for 0% -> 0%
where the time goes in v1:
time: 36.4 us; the launch traced here: 36.2 us
  Pallas kernels  33.7 us (93%)
  local copies, waits for them, and re-layouts  1.88 us (5%)
  between operations  0.65 us (2%)
    pallas_call x1, Pallas kernels, step(): pl.pallas_call(functools.partial(body, (cells, grps, na, ng, nb, nq, nm))...  33.7 us
    unnamed x4, local copies, waits for them, and re-layouts  1.88 us

profile of v1, /device:TPU:0, one launch (start us, length us, event | category | flops | bytes accessed | tf_op | source)
XLA Modules:
  0.0 36.2 jit_solution(11165605319143148816)
XLA Ops:
  0.6 33.7 %shard_map.113 = (f32[3,512]{1,0:T(4,128)}, f32[384]{0:T(512)}) custom-call(s32[4,8]{1,0:T(4,128)} %refs_0_.1, s32[4,4]{1,0:T(4,128)} %refs_1_.1, s32[3,8]{1,0:T(4,128)} %refs_2_.1, f32[3,512]{1,0:T(4,128)} %refs_3_.1, f32[3,384]{1,0:T(4,128)} %refs_4_.1, f32[3,512]{1,0:T(4,128)} %refs_5_.1, f32[3,512]{1,0:T(4,128)} %refs_6_.1, f32[512]{0:T(512)} %refs_7_.1, ...), custom_call_target="tpu_custom_call" | custom-call | tf_op jit(solution)/shard_map/pallas_call | solution.py:433
  34.3 0.0 copy-start
  34.3 1.3 %copy.14 = f32[3,512]{1,0:T(4,128)} copy(f32[3,512]{1,0:T(4,128)} %get-tuple-element.4) | data formatting | bytes 12288
  35.6 0.0 copy-done
  35.6 0.6 %copy.15 = f32[384]{0:T(512)} copy(f32[384]{0:T(512)S(1)} %copy-done) | data formatting | bytes 3072
Async XLA Ops:
  34.3 1.3 %copy-start = (f32[384]{0:T(512)S(1)}, f32[384]{0:T(512)}, u32[]{:S(2)}) copy-start(f32[384]{0:T(512)} %get-tuple-element.5) | copy-start | bytes 4612

commit v2 on v1

--- a/solution.py
+++ b/solution.py
@@ -25,14 +25,14 @@
 
 def body(dims, *refs):
     cells, grps, na, ng, nb, nq, nm = dims
-    near_s, grid_s, source_s, sites, points, guess, fixed, pol, base, resp = refs[:10]
-    out_dip, out_q = refs[10:12]
-    stat = refs[12]
-    dyn = refs[13 : 13 + ITERS]
-    tab = refs[13 + ITERS : 13 + 2 * ITERS]
-    rest = refs[13 + 2 * ITERS :]
+    args, (out_dip, out_q), held = refs[:10], refs[10:12], refs[12:22]
+    near_s, grid_s, source_s, sites, points, guess, fixed, pol, base, resp = held
+    stat = refs[22]
+    dyn = refs[23 : 23 + ITERS]
+    tab = refs[23 + ITERS : 23 + 2 * ITERS]
+    rest = refs[23 + 2 * ITERS :]
     tgt_a, tgt_g, geo, cgeo, pgeo, fld = rest[:6]
-    stat_send, stat_recv, dyn_send, dyn_recv, far_send, far_recv = rest[6:]
+    load_sem, stat_send, stat_recv, dyn_send, dyn_recv, far_send, far_recv = rest[6:]
     cell = lax.axis_index("cell")
     grp = lax.axis_index("grp")
     has_prev = cell > 0
@@ -74,30 +74,27 @@
     def greet(c, g):
         pl.semaphore_signal(barrier, inc=1, device_id=(c, g), device_id_type=MESH)
 
-    def each_far(act):
-        def step(c, carry):
-            @pl.when(jnp.abs(c - cell) >= 2)
-            def _():
-                act(c)
-
+    def each_other_cell(act):
+        def step(n, carry):
+            c = lax.rem(cell + n, cells)
+            for d in range(grps):
+                act(c, lax.rem(grp + d, grps))
             return carry
 
-        lax.fori_loop(0, cells, step, 0)
-
-    each_far(lambda c: greet(c, grp))
-
-    @pl.when(has_prev)
-    def _():
-        for j in range(grps):
-            greet(cell - 1, j)
-
-    @pl.when(has_next)
-    def _():
-        for j in range(grps):
-            greet(cell + 1, j)
-
+        lax.fori_loop(1, cells, step, 0)
+
+    each_other_cell(greet)
     for d in range(1, grps):
         greet(cell, lax.rem(grp + d, grps))
+
+    loads = [
+        pltpu.make_async_copy(src, dst, load_sem.at[n])
+        for n, (src, dst) in enumerate(zip(args, held))
+    ]
+    for load in loads:
+        load.start()
+    for load in loads:
+        load.wait()
 
     for a in range(3):
         for b in range(na):
@@ -136,6 +133,9 @@
         ref[slot + 1] = dy * cube
         ref[slot + 2] = dz * cube
 
+    def column_sum(x):
+        return jnp.sum(x, axis=0, keepdims=True)
+
     def wide(row):
         return jnp.broadcast_to(row, (SUB, BLOCK))
 
@@ -148,10 +148,7 @@
             slot = (b * GROUPS + t) * nk * 4
             store_dipole_pair(slot, targets_of(tgt_a, b, t), source, diag == t * SUB)
 
-    greeted = grps - 1
-    greeted += has_prev.astype(jnp.int32) * (grps - 1) + has_next.astype(jnp.int32) * (grps - 1)
-    greeted += cells - 1
-    pl.semaphore_wait(barrier, greeted)
+    pl.semaphore_wait(barrier, cells * grps - 1)
 
     def piece_copy(buf, send, recv, slot, c, g):
         return pltpu.make_async_remote_copy(
@@ -210,47 +207,49 @@
     def start(copy):
         copy.start()
 
-    def far_copy(it, c):
+    def far_row(it, c, g):
+        return tab[it].at[pl.ds(g * cells + c, 1)]
+
+    def far_copy(it, c, g):
         return pltpu.make_async_remote_copy(
-            src_ref=tab[it].at[cell],
-            dst_ref=tab[it].at[cell],
-            send_sem=far_send.at[it, c],
-            recv_sem=far_recv.at[it, cell],
-            device_id=(c, grp),
+            src_ref=far_row(it, cell, grp),
+            dst_ref=far_row(it, cell, grp),
+            send_sem=far_send.at[it],
+            recv_sem=far_recv.at[it],
+            device_id=(c, g),
             device_id_type=MESH,
         )
 
-    def far_arrival(it, c):
-        pltpu.make_async_remote_copy(
-            src_ref=tab[it].at[c],
-            dst_ref=tab[it].at[c],
-            send_sem=far_send.at[it, c],
-            recv_sem=far_recv.at[it, c],
-            device_id=(c, grp),
+    def far_all(it):
+        rows = tab[it].at[pl.ds(0, (cells - 1) * grps)]
+        return pltpu.make_async_remote_copy(
+            src_ref=rows,
+            dst_ref=rows,
+            send_sem=far_send.at[it],
+            recv_sem=far_recv.at[it],
+            device_id=(lax.rem(cell + 1, cells), grp),
             device_id_type=MESH,
-        ).wait_recv()
-
-    def cell_sums(it):
-        rows = []
-        total = dyn[it][grps]
-        for p in range(1, grps):
-            total = total + dyn[it][grps + p]
+        )
+
+    def own_sums(it):
+        mine = dyn[it][own]
+        rows = [column_sum(mine[a * na : (a + 1) * na]) for a in range(3)]
+        q = mine[3 * na : 3 * na + ng]
+        rows.append(column_sum(q))
         for a in range(3):
-            rows.append(jnp.sum(total[a * na : (a + 1) * na], axis=0, keepdims=True))
-        rows.append(jnp.sum(total[3 * na : 3 * na + ng], axis=0, keepdims=True))
-        for a in range(3):
-            moment = None
-            for p in range(grps):
-                q = dyn[it][grps + p, 3 * na : 3 * na + ng, :]
-                r = 3 * na + a * ng
-                term = q * (stat[grps + p, r : r + ng, :] - centre[a])
-                moment = term if moment is None else moment + term
-            rows.append(jnp.sum(moment, axis=0, keepdims=True))
+            r = 3 * na + a * ng
+            rows.append(column_sum(q * (stat[own, r : r + ng, :] - centre[a])))
         tile = jnp.zeros((SUB, BLOCK), jnp.float32)
         for n, row in enumerate(rows):
             tile = jnp.where(subs == n, wide(row), tile)
         sums = jnp.sum(tile, axis=1, keepdims=True)
-        tab[it][cell] = jnp.broadcast_to(sums, (SUB, BLOCK))
+        tab[it][grp * cells + cell] = column_sum(jnp.where(diag == 0, sums, 0.0))
+
+    def far_sums(it):
+        total = tab[it][0:cells, 0, :]
+        for g in range(1, grps):
+            total = total + tab[it][g * cells : (g + 1) * cells, 0, :]
+        return [jnp.broadcast_to(total[:, n : n + 1], (cells, BLOCK)) for n in range(7)]
 
     def mm_place(w):
         return lax.div(w, na), lax.rem(w, na)
@@ -351,32 +350,29 @@
         cube = jnp.where(jnp.abs(c - cell) >= 2, inv * inv * inv, 0.0)
         return (dx, dy, dz), cube, cube * inv * inv * 3.0
 
-    def column_sum(x):
-        return jnp.sum(x, axis=0, keepdims=True)
-
     for_peers(stat, stat_send, stat_recv, start)
     for_peers(dyn[0], dyn_send.at[0], dyn_recv.at[0], start)
     for_neighbours(stat, stat_send, stat_recv, start)
     for_neighbours(dyn[0], dyn_send.at[0], dyn_recv.at[0], start)
-    peers_arrive(stat, stat_send, stat_recv)
 
     for it in range(ITERS):
         send, recv = dyn_send.at[it], dyn_recv.at[it]
         if it > 0:
             for_peers(dyn[it], send, recv, start)
             for_neighbours(dyn[it], send, recv, start)
-        peers_arrive(dyn[it], send, recv)
-        cell_sums(it)
-        each_far(lambda c: far_copy(it, c).start())
+        own_sums(it)
+        each_other_cell(lambda c, g: far_copy(it, c, g).start())
         if it == 0:
+            peers_arrive(stat, stat_send, stat_recv)
             neighbours_arrive(stat, stat_send, stat_recv)
             lax.fori_loop(0, na * HALVES, geometry_atoms, 0)
             lax.fori_loop(0, ng * HALVES, geometry_grid, 0)
+        peers_arrive(dyn[it], send, recv)
         neighbours_arrive(dyn[it], send, recv)
         lax.fori_loop(0, na * HALVES, functools.partial(near_atoms, it), 0)
         lax.fori_loop(0, ng * HALVES, functools.partial(near_grid, it), 0)
-        each_far(lambda c: far_arrival(it, c))
-        sums = [tab[it][:, n, :] for n in range(7)]
+        far_all(it).wait_recv()
+        sums = far_sums(it)
         moments = [sums[a] + sums[4 + a] for a in range(3)]
         for b in range(na):
             delta, cube, fifth = far_geometry(lambda a: vec_row(sites, a, b))
@@ -414,7 +410,7 @@
     for it in range(ITERS):
         for_peers(dyn[it], dyn_send.at[it], dyn_recv.at[it], finish)
         for_neighbours(dyn[it], dyn_send.at[it], dyn_recv.at[it], finish)
-        each_far(lambda c: far_copy(it, c).wait_send())
+        far_all(it).wait_send()
 
 
 def solution(mesh):
@@ -427,7 +423,7 @@
         stat_rows = round_up(3 * na + 3 * ng, SUB)
         dyn_rows = round_up(3 * na + ng, SUB)
         f32 = jnp.float32
-        smem = pl.BlockSpec(memory_space=pltpu.SMEM)
+        args = (near, grid, source, sites, points, guess, fixed, pol, base, resp)
         vmem = pl.BlockSpec(memory_space=pltpu.VMEM)
         dma = pltpu.SemaphoreType.DMA
         return pl.pallas_call(
@@ -436,11 +432,13 @@
                 jax.ShapeDtypeStruct(sites.shape, f32),
                 jax.ShapeDtypeStruct(base.shape, f32),
             ),
-            in_specs=[smem] * 3 + [vmem] * 7,
+            in_specs=[pl.BlockSpec(memory_space=pl.ANY)] * 10,
             out_specs=(vmem, vmem),
-            scratch_shapes=[pltpu.VMEM((3 * grps, stat_rows, BLOCK), f32)]
+            scratch_shapes=[pltpu.SMEM(x.shape, x.dtype) for x in args[:3]]
+            + [pltpu.VMEM(x.shape, x.dtype) for x in args[3:]]
+            + [pltpu.VMEM((3 * grps, stat_rows, BLOCK), f32)]
             + [pltpu.VMEM((3 * grps, dyn_rows, BLOCK), f32) for _ in range(ITERS)]
-            + [pltpu.VMEM((cells, SUB, BLOCK), f32) for _ in range(ITERS)]
+            + [pltpu.VMEM((cells * grps, 1, BLOCK), f32) for _ in range(ITERS)]
             + [
                 pltpu.VMEM((na, 3, BLOCK, BLOCK), f32),
                 pltpu.VMEM((ng, 3, BLOCK, BLOCK), f32),
@@ -448,15 +446,16 @@
                 pltpu.VMEM((na * GROUPS * nq * 3, SUB, BLOCK), f32),
                 pltpu.VMEM((ng * GROUPS * nm * 3, SUB, BLOCK), f32),
                 pltpu.VMEM(((na * 3 + ng) * HALVES, SUB, BLOCK), f32),
+                dma((10,)),
                 dma((3 * grps,)),
                 dma((3 * grps,)),
                 dma((ITERS, 3 * grps)),
                 dma((ITERS, 3 * grps)),
-                dma((ITERS, cells)),
-                dma((ITERS, cells)),
+                dma((ITERS,)),
+                dma((ITERS,)),
             ],
             compiler_params=pltpu.CompilerParams(collective_id=0, has_side_effects=True),
-        )(near, grid, source, sites, points, guess, fixed, pol, base, resp)
+        )(*args)
 
     pair = P(("cell", "grp"))
     wide = P(None, ("cell", "grp"))

time: 36.4 us -> 36 us (0.989)
  Pallas kernels: 33.7 us -> 33.2 us
    pallas_call x1, Pallas kernels: 33.7 us -> 33.2 us  [step(): pl.pallas_call(functools.partial(body, (cells, grps, na, ng, nb, nq, nm))...]
where the time goes in v2:
time: 36 us; the launch traced here: 35.8 us
  Pallas kernels  33.2 us (92%)
  local copies, waits for them, and re-layouts  1.88 us (5%)
  between operations  0.65 us (2%)
    pallas_call x1, Pallas kernels, step(): pl.pallas_call(functools.partial(body, (cells, grps, na, ng, nb, nq, nm))...  33.2 us
    unnamed x4, local copies, waits for them, and re-layouts  1.88 us

profile of v2, /device:TPU:0, one launch (start us, length us, event | category | flops | bytes accessed | tf_op | source)
XLA Modules:
  0.0 35.8 jit_solution(3207228217302466780)
XLA Ops:
  0.6 33.2 %shard_map.113 = (f32[3,512]{1,0:T(4,128)}, f32[384]{0:T(512)}) custom-call(s32[4,8]{1,0:T(4,128)} %refs_0_.1, s32[4,4]{1,0:T(4,128)} %refs_1_.1, s32[3,8]{1,0:T(4,128)} %refs_2_.1, f32[3,512]{1,0:T(4,128)} %refs_3_.1, f32[3,384]{1,0:T(4,128)} %refs_4_.1, f32[3,512]{1,0:T(4,128)} %refs_5_.1, f32[3,512]{1,0:T(4,128)} %refs_6_.1, f32[512]{0:T(512)} %refs_7_.1, ...), custom_call_target="tpu_custom_call" | custom-call | tf_op jit(solution)/shard_map/pallas_call | solution.py:429
  33.9 0.0 copy-start
  33.9 1.3 %copy.14 = f32[3,512]{1,0:T(4,128)} copy(f32[3,512]{1,0:T(4,128)} %get-tuple-element.4) | data formatting | bytes 12288
  35.2 0.0 copy-done
  35.2 0.6 %copy.15 = f32[384]{0:T(512)} copy(f32[384]{0:T(512)S(1)} %copy-done) | data formatting | bytes 3072
Async XLA Ops:
  33.9 1.3 %copy-start = (f32[384]{0:T(512)S(1)}, f32[384]{0:T(512)}, u32[]{:S(2)}) copy-start(f32[384]{0:T(512)} %get-tuple-element.5) | copy-start | bytes 4612

commit v3 on v2

--- a/solution.py
+++ b/solution.py
@@ -31,8 +31,8 @@
     dyn = refs[23 : 23 + ITERS]
     tab = refs[23 + ITERS : 23 + 2 * ITERS]
     rest = refs[23 + 2 * ITERS :]
-    tgt_a, tgt_g, geo, cgeo, pgeo, fld = rest[:6]
-    load_sem, stat_send, stat_recv, dyn_send, dyn_recv, far_send, far_recv = rest[6:]
+    tgt_a, tgt_g, geo, cgeo, pgeo, fld, selfs = rest[:7]
+    load_sem, stat_send, stat_recv, dyn_send, dyn_recv, far_send, far_recv = rest[7:]
     cell = lax.axis_index("cell")
     grp = lax.axis_index("grp")
     has_prev = cell > 0
@@ -290,12 +290,24 @@
                 store_charge_pair(pgeo, slot, targets_of(tgt_g, b, first + t), source)
         return carry
 
+    def self_atoms(it, i, carry):
+        b = lax.div(i, HALVES)
+        mu = [wide(dyn[it][own, pl.ds(a * na + b, 1), :]) for a in range(3)]
+        for t in range(UNROLL):
+            slot = (i * UNROLL + t) * nk * 4
+            u = [geo[slot + a] for a in range(3)]
+            cube = geo[slot + 3]
+            proj = u[0] * mu[0] + u[1] * mu[1] + u[2] * mu[2]
+            for a in range(3):
+                selfs[(i * UNROLL + t) * 3 + a] = u[a] * proj - cube * mu[a]
+        return carry
+
     def near_atoms(it, i, carry):
         b = lax.div(i, HALVES)
         first = lax.rem(i, HALVES) * UNROLL
-        acc = [[None] * 3 for _ in range(UNROLL)]
-        for k in range(nk):
-            p, lb = (own, b) if k == 0 else mm_place(near_s[b, k - 1])
+        acc = [[selfs[(i * UNROLL + t) * 3 + a] for a in range(3)] for t in range(UNROLL)]
+        for k in range(1, nk):
+            p, lb = mm_place(near_s[b, k - 1])
             mu = [wide(dyn[it][p, pl.ds(a * na + lb, 1), :]) for a in range(3)]
             for t in range(UNROLL):
                 slot = ((i * UNROLL + t) * nk + k) * 4
@@ -304,7 +316,7 @@
                 proj = u[0] * mu[0] + u[1] * mu[1] + u[2] * mu[2]
                 for a in range(3):
                     term = u[a] * proj - cube * mu[a]
-                    acc[t][a] = term if k == 0 else acc[t][a] + term
+                    acc[t][a] = acc[t][a] + term
         for k in range(nq):
             p, lb = grid_place(grid_s[b, k])
             q = wide(dyn[it][p, pl.ds(3 * na + lb, 1), :])
@@ -350,18 +362,19 @@
         cube = jnp.where(jnp.abs(c - cell) >= 2, inv * inv * inv, 0.0)
         return (dx, dy, dz), cube, cube * inv * inv * 3.0
 
+    for_neighbours(stat, stat_send, stat_recv, start)
     for_peers(stat, stat_send, stat_recv, start)
+    for_neighbours(dyn[0], dyn_send.at[0], dyn_recv.at[0], start)
     for_peers(dyn[0], dyn_send.at[0], dyn_recv.at[0], start)
-    for_neighbours(stat, stat_send, stat_recv, start)
-    for_neighbours(dyn[0], dyn_send.at[0], dyn_recv.at[0], start)
 
     for it in range(ITERS):
         send, recv = dyn_send.at[it], dyn_recv.at[it]
         if it > 0:
+            for_neighbours(dyn[it], send, recv, start)
             for_peers(dyn[it], send, recv, start)
-            for_neighbours(dyn[it], send, recv, start)
         own_sums(it)
         each_other_cell(lambda c, g: far_copy(it, c, g).start())
+        lax.fori_loop(0, na * HALVES, functools.partial(self_atoms, it), 0)
         if it == 0:
             peers_arrive(stat, stat_send, stat_recv)
             neighbours_arrive(stat, stat_send, stat_recv)
@@ -446,6 +459,7 @@
                 pltpu.VMEM((na * GROUPS * nq * 3, SUB, BLOCK), f32),
                 pltpu.VMEM((ng * GROUPS * nm * 3, SUB, BLOCK), f32),
                 pltpu.VMEM(((na * 3 + ng) * HALVES, SUB, BLOCK), f32),
+                pltpu.VMEM((na * GROUPS * 3, SUB, BLOCK), f32),
                 dma((10,)),
                 dma((3 * grps,)),
                 dma((3 * grps,)),

time: 36 us -> 35.4 us (0.983)
  Pallas kernels: 33.2 us -> 32.7 us
    pallas_call x1, Pallas kernels: 33.2 us -> 32.7 us  [step(): pl.pallas_call(functools.partial(body, (cells, grps, na, ng, nb, nq, nm))...]
where the time goes in v3:
time: 35.4 us; the launch traced here: 35.2 us
  Pallas kernels  32.7 us (92%)
  local copies, waits for them, and re-layouts  1.88 us (5%)
  between operations  0.65 us (2%)
    pallas_call x1, Pallas kernels, step(): pl.pallas_call(functools.partial(body, (cells, grps, na, ng, nb, nq, nm))...  32.7 us
    unnamed x4, local copies, waits for them, and re-layouts  1.88 us

profile of v3, /device:TPU:0, one launch (start us, length us, event | category | flops | bytes accessed | tf_op | source)
XLA Modules:
  0.0 35.2 jit_solution(2625388677620601132)
XLA Ops:
  0.6 32.7 %shard_map.113 = (f32[3,512]{1,0:T(4,128)}, f32[384]{0:T(512)}) custom-call(s32[4,8]{1,0:T(4,128)} %refs_0_.1, s32[4,4]{1,0:T(4,128)} %refs_1_.1, s32[3,8]{1,0:T(4,128)} %refs_2_.1, f32[3,512]{1,0:T(4,128)} %refs_3_.1, f32[3,384]{1,0:T(4,128)} %refs_4_.1, f32[3,512]{1,0:T(4,128)} %refs_5_.1, f32[3,512]{1,0:T(4,128)} %refs_6_.1, f32[512]{0:T(512)} %refs_7_.1, ...), custom_call_target="tpu_custom_call" | custom-call | tf_op jit(solution)/shard_map/pallas_call | solution.py:442
  33.4 0.0 copy-start
  33.4 1.3 %copy.14 = f32[3,512]{1,0:T(4,128)} copy(f32[3,512]{1,0:T(4,128)} %get-tuple-element.4) | data formatting | bytes 12288
  34.7 0.0 copy-done
  34.7 0.6 %copy.15 = f32[384]{0:T(512)} copy(f32[384]{0:T(512)S(1)} %copy-done) | data formatting | bytes 3072
Async XLA Ops:
  33.4 1.3 %copy-start = (f32[384]{0:T(512)S(1)}, f32[384]{0:T(512)}, u32[]{:S(2)}) copy-start(f32[384]{0:T(512)} %get-tuple-element.5) | copy-start | bytes 4612
